TPU v7x, 256 devices: a whole 4x4x8 slice. The times are simulated.
256 devices in a mesh: dp: 16 (over y, x_hi, core), tensor: 16 (over x_lo, z).
Axes of the slice: x: 4 (x_hi: 2, x_lo: 2; x = x_hi * 2 + x_lo), y: 4, z: 8, core: 2. Of those that a mesh axis runs over, the one named last changes fastest.
Arguments:
- tokens: bfloat16 [32768, 2304], P(('dp', 'tensor')), may hold values from -6 to 6
- cotangent: bfloat16 [32768, 4096], P('dp', 'tensor'), may hold values from -6 to 6
- pre_gain: float32 [2304], replicated, may hold values from 0.25 to 1.75
- w_query: bfloat16 [2304, 4096], P('dp', 'tensor'), may hold values from -0.375 to 0.375
- key_weight: bfloat16 [2304, 2048], P('dp', 'tensor'), may hold values from -0.375 to 0.375
- value_weight: bfloat16 [2304, 2048], P('dp', 'tensor'), may hold values from -0.125 to 0.125
Outputs:
- attended: bfloat16 [32768, 4096], P('dp', 'tensor')
- grad_tokens: bfloat16 [32768, 2304], P(('dp', 'tensor'))
- grad_query: float32 [2304, 4096], P('dp', 'tensor')
- grad_key: float32 [2304, 2048], P('dp', 'tensor')
- grad_value: float32 [2304, 2048], P('dp', 'tensor')
- grad_pre_gain: float32 [2304], replicated
All inputs are finite; a program needn't handle non-finite values.
Results may differ from a plain program's by a relative error of at most 0.019.
The roundings to bfloat16 on the way count: a program that leaves them out, or rounds other values in their place, can miss the bound.
Values may be sent and summed in bfloat16 or wider, within the bound.
No kernel may reach another device: no remote copies, remote signals or barrier semaphores. Data moves between devices by JAX's collectives and lax.ppermute only.
A program may use at most 192 MiB of HBM per device.

v0:
```python
import functools
import jax
import jax.numpy as jnp
from jax import lax
from jax.sharding import Mesh
from jax.sharding import PartitionSpec as P

HEAD_SIZE = 128
SEQ_LEN = 64
TENSOR = ("tensor_0", "tensor_1")
DP = ("dp_0", "dp_1", "dp_2")
DP_TENSOR = ("dp_0", "dp_1", "dp_2", "tensor_0", "tensor_1")
EPS = 1e-06
CAP = 50.0
BASE = 10000.0
query_scalar = 144.0


def in_one_piece(arrays, axis, dim, along):
    widths = [a.shape[along] for a in arrays]
    both = jnp.concatenate(arrays, axis=along)
    result = lax.all_gather(both, axis, axis=dim, tiled=True)
    return tuple(jnp.split(result, [sum(widths[:k]) for k in range(1, len(widths))], axis=along))


def split_up(value, dim, devices):
    before, after = (value.shape[:dim], value.shape[dim + 1 :])
    return jnp.moveaxis(value.reshape(*before, devices, -1, *after), dim, 0)


def sum_at_owner(value, axis, dim):
    devices = lax.axis_size(axis)
    parts = lax.all_to_all(split_up(value, dim, devices), axis, 0, 0, tiled=True)
    return jnp.sum(parts.astype(jnp.float32), axis=0)


def one_axis_at_a_time(value, axes):
    return functools.reduce(lax.psum, axes, value)


def rotary_tables(segment_length, half):
    places = jnp.arange(segment_length, dtype=jnp.float32)[:, None]
    freqs = BASE ** (-jnp.arange(half, dtype=jnp.float32) / half)
    angles = places * freqs[None, :]
    return (jnp.cos(angles)[:, None, :], jnp.sin(angles)[:, None, :])


def rotate(values, cosine_table, sine_table):
    half = values.shape[-1] // 2
    first, second = (values[..., :half], values[..., half:])
    return jnp.concatenate(
        [first * cosine_table - second * sine_table, second * cosine_table + first * sine_table], -1
    )


def inverse_rotation(values, cosine_table, sine_table):
    half = values.shape[-1] // 2
    first, second = (values[..., :half], values[..., half:])
    return jnp.concatenate(
        [first * cosine_table + second * sine_table, second * cosine_table - first * sine_table], -1
    )


def attend_forward(query, key, value):
    repeat = query.shape[1] // key.shape[1]
    keys = jnp.repeat(key, repeat, axis=1)
    values = jnp.repeat(value, repeat, axis=1)
    factor = query_scalar ** (-0.5)
    raw = jnp.einsum("qhd,khd->hqk", query, keys, preferred_element_type=jnp.float32) * factor
    bent = jnp.tanh(raw / CAP)
    capped = CAP * bent
    segment_length = query.shape[0]
    causal = jnp.arange(segment_length)[None, :] <= jnp.arange(segment_length)[:, None]
    raised = jnp.where(causal[None], jnp.exp(capped), 0.0)
    weights = raised / jnp.sum(raised, -1, keepdims=True)
    probs = weights.astype(jnp.bfloat16)
    attended = jnp.einsum("hqk,khd->qhd", probs, values, preferred_element_type=jnp.float32).astype(
        jnp.bfloat16
    )
    return (attended, weights, probs, bent)


def attend_backward(d_attended, query, key, value, weights, probs, bent):
    repeat = query.shape[1] // key.shape[1]
    keys = jnp.repeat(key, repeat, axis=1)
    values = jnp.repeat(value, repeat, axis=1)
    factor = query_scalar ** (-0.5)
    d_probs = jnp.einsum("qhd,khd->hqk", d_attended, values, preferred_element_type=jnp.float32)
    d_capped = weights * (d_probs - jnp.sum(weights * d_probs, -1, keepdims=True))
    d_scores = (d_capped * (1.0 - bent * bent) * factor).astype(jnp.bfloat16)
    query_back = jnp.einsum("hqk,khd->qhd", d_scores, keys, preferred_element_type=jnp.float32)
    key_heads = jnp.einsum("hqk,qhd->khd", d_scores, query, preferred_element_type=jnp.float32)
    value_heads = jnp.einsum("hqk,qhd->khd", probs, d_attended, preferred_element_type=jnp.float32)
    segment_length, heads, width = query.shape
    key_rotated_back = key_heads.reshape(segment_length, heads // repeat, repeat, width).sum(2)
    value_returned = value_heads.reshape(segment_length, heads // repeat, repeat, width).sum(2)
    return (query_back, key_rotated_back, value_returned)


def segment_pass(query, key, value, d_attended):
    attended, weights, probs, bent = attend_forward(query, key, value)
    query_back, key_rotated_back, value_returned = attend_backward(
        d_attended, query, key, value, weights, probs, bent
    )
    return (attended, query_back, key_rotated_back, value_returned)


def per_device(tokens, cotangent, pre_gain, w_query, key_weight, value_weight):
    contract_first = (((0,), (0,)), ((), ()))
    contract_last = (((1,), (1,)), ((), ()))
    rows_f = tokens.astype(jnp.float32)
    inv_one = lax.rsqrt(jnp.mean(rows_f * rows_f, -1, keepdims=True) + EPS)
    unit_one = rows_f * inv_one
    normed_input = (unit_one * pre_gain).astype(jnp.bfloat16)
    gathered = lax.all_gather(normed_input, TENSOR, axis=0, tiled=True)
    segment_length = gathered.shape[0]
    token_span = SEQ_LEN
    pieces_count = segment_length // token_span
    heads_query = w_query.shape[1] // HEAD_SIZE
    heads_key = key_weight.shape[1] // HEAD_SIZE
    pieces = in_one_piece((w_query, key_weight, value_weight), DP, 0, 1)
    query_raw, key_unrotated, value_projected = tuple(
        (jnp.dot(gathered, piece, preferred_element_type=jnp.float32) for piece in pieces)
    )
    cosine_table, sine_table = rotary_tables(token_span, HEAD_SIZE // 2)
    query = rotate(
        query_raw.reshape(pieces_count, token_span, heads_query, HEAD_SIZE),
        cosine_table,
        sine_table,
    ).astype(jnp.bfloat16)
    key = rotate(
        key_unrotated.reshape(pieces_count, token_span, heads_key, HEAD_SIZE),
        cosine_table,
        sine_table,
    ).astype(jnp.bfloat16)
    value = value_projected.reshape(pieces_count, token_span, heads_key, HEAD_SIZE).astype(
        jnp.bfloat16
    )
    d_attended = cotangent.reshape(pieces_count, token_span, heads_query, HEAD_SIZE)
    attended, query_back, key_rotated_back, value_returned = jax.vmap(segment_pass)(
        query, key, value, d_attended
    )
    attended_flat = attended.reshape(segment_length, heads_query * HEAD_SIZE)
    d_query = (
        inverse_rotation(query_back, cosine_table, sine_table)
        .astype(jnp.bfloat16)
        .reshape(segment_length, heads_query * HEAD_SIZE)
    )
    key_gradient = (
        inverse_rotation(key_rotated_back, cosine_table, sine_table)
        .astype(jnp.bfloat16)
        .reshape(segment_length, heads_key * HEAD_SIZE)
    )
    value_gradient = value_returned.astype(jnp.bfloat16).reshape(
        segment_length, heads_key * HEAD_SIZE
    )
    back_query, back_key, back_value = in_one_piece((w_query, key_weight, value_weight), DP, 0, 1)
    joined = jnp.concatenate([d_query, key_gradient, value_gradient], 1)
    block = gathered
    grads = sum_at_owner(
        lax.dot_general(block, joined, contract_first, preferred_element_type=jnp.float32).astype(
            jnp.bfloat16
        ),
        DP,
        0,
    )
    width_query = w_query.shape[1]
    width_key = key_weight.shape[1]
    grad_query = grads[:, :width_query]
    grad_key = grads[:, width_query : width_query + width_key]
    grad_value = grads[:, width_query + width_key :]
    total = jnp.zeros((tokens.shape[0] * lax.axis_size(TENSOR), gathered.shape[1]), jnp.float32)
    for grad_part, weight in (
        (d_query, back_query),
        (key_gradient, back_key),
        (value_gradient, back_value),
    ):
        block = grad_part
        total = total + lax.dot_general(
            block, weight, contract_last, preferred_element_type=jnp.float32
        )
    d_normed = lax.psum_scatter(
        total.astype(jnp.bfloat16), TENSOR, scatter_dimension=0, tiled=True
    ).astype(jnp.float32)
    pre_part = jnp.sum(d_normed * unit_one, 0)
    scaled_in = d_normed * pre_gain
    grad_tokens = (
        inv_one * (scaled_in - unit_one * jnp.mean(scaled_in * unit_one, -1, keepdims=True))
    ).astype(jnp.bfloat16)
    grad_pre = one_axis_at_a_time(pre_part, DP_TENSOR)
    return (attended_flat, grad_tokens, grad_query, grad_key, grad_value, grad_pre)


def solution(mesh):
    torus = Mesh(
        mesh.devices.reshape(4, 2, 2, 2, 8), ("dp_0", "dp_1", "dp_2", "tensor_0", "tensor_1")
    )
    in_specs = (P(DP_TENSOR, None), P(DP, TENSOR), P(), P(DP, TENSOR), P(DP, TENSOR), P(DP, TENSOR))
    out_specs = (
        P(DP, TENSOR),
        P(DP_TENSOR, None),
        P(DP, TENSOR),
        P(DP, TENSOR),
        P(DP, TENSOR),
        P(),
    )
    return jax.shard_map(
        per_device, mesh=torus, in_specs=in_specs, out_specs=out_specs, check_vma=False
    )
```

profile of v0, /device:TPU:4, one launch (start us, length us, event | category | flops | bytes accessed | tf_op | source)
XLA Modules:
  0.0 471.2 jit_solution(14125155676329583121)
XLA Ops:
  7.2 0.0 copy-start.11
  7.2 0.0 all-gather.5.cloned.1.call-start
  7.2 1.7 pad_maximum_fusion.5
  8.9 0.0 all-gather.5.cloned.1.call-update
  8.9 0.0 all-gather.3.cloned.1.call-start
  9.0 1.3 fusion.24
  10.3 2.1 fusion.22
  12.3 0.0 all-gather.3.cloned.1.call-update
  12.4 0.0 reduce-scatter.2.cloned.1.call-start
  12.4 0.0 copy-done.11
  12.4 0.3 reshape.135
  12.8 0.1 fusion.53
  12.9 52.2 %all-gather.5.cloned.1.call-done = bf16[2304,512]{1,0:T(8,128)(2,1)} async-done(((bf16[144,512]{1,0:T(8,128)(2,1)}), bf16[2304,512]{1,0:T(8,128)(2,1)}) %all-gather.5.cloned.1.call-update) | async-done | bytes 2359312 | tf_op jit(solution)/shard_map/all_gather | solution.py:22
  65.1 114.8 %all-gather.3.cloned.1.call-done = bf16[2048,2304]{1,0:T(8,128)(2,1)} async-done(((bf16[128,2304]{1,0:T(8,128)(2,1)}), bf16[2048,2304]{1,0:T(8,128)(2,1)}) %all-gather.3.cloned.1.call-update) | async-done | bytes 9437200 | tf_op jit(solution)/shard_map/all_gather | solution.py:115
  179.9 7.9 %fusion.28 = f32[2048,256]{1,0:T(8,128)} fusion(bf16[2048,2304]{1,0:T(8,128)(2,1)} %all-gather.3.cloned.1.call-done, bf16[2304,512]{1,0:T(8,128)(2,1)} %all-gather.5.cloned.1.call-done), kind=kOutput, calls=%fused_computation.56 | convolution fusion | flops 2415919104 | bytes 12713984 | tf_op jit(solution)/shard_map/dot_general | solution.py:123
  187.8 2.3 reshape.131
  190.1 0.0 slice-start
  190.1 2.4 fusion.72
  192.6 0.0 slice-start.1
  192.6 0.0 slice-start.2
  192.6 6.3 %fusion.48 = f32[2048,128]{1,0:T(8,128)S(1)} fusion(bf16[2048,2304]{1,0:T(8,128)(2,1)} %all-gather.3.cloned.1.call-done, bf16[2304,512]{1,0:T(8,128)(2,1)S(1)} %copy-done.2), kind=kOutput, calls=%fused_computation.77 | convolution fusion | flops 1207959552 | bytes 11075584 | tf_op jit(solution)/shard_map/dot_general | solution.py:123
  198.9 0.4 fusion.34
  199.4 0.3 pad_maximum_fusion.2
  199.7 2.7 convolution_convert_fusion.1
  202.4 0.0 copy-start.13
  202.5 0.7 fusion.32
  203.1 0.1 copy-done.13
  203.2 0.7 subtract_convert_fusion.1
  203.9 0.0 copy-start.10
  204.0 2.6 fusion.13
  206.6 6.2 %convolution_bitcast_fusion.2 = f32[32,64,1,128]{3,1,0,2:T(8,128)} fusion(f32[32,2,64,64]{3,2,1,0:T(8,128)S(1)} %fusion.32, f32[32,2,64,64]{2,3,1,0:T(8,128)} %get-tuple-element.23, bf16[32,64,2,64]{3,1,2,0:T(8,128)(2,1)} %copy-done.10, bf16[32,64,2,64]{3,1,2,0:T(8,128)(2,1)} %copy-done.9, f32[32,2,64]{2,1,0:T(2,128)S(1)} %get-tuple-element.22, ...), kind=kOutput, calls=%fused_computation.38 | convolution fusion | flops 73404480 | bytes 4214784 | tf_op jit(solution)/shard_map/vmap(hqk,qhd->khd)/dot_general | solution.py:92
  212.8 6.3 %convolution_bitcast_fusion = f32[32,64,2,128]{3,1,2,0:T(8,128)S(1)} fusion(f32[32,2,64,64]{3,2,1,0:T(8,128)} %copy-done.8, f32[32,2,64,64]{2,3,1,0:T(8,128)} %get-tuple-element.23, bf16[32,64,128]{2,1,0:T(8,128)(2,1)} %copy-done.15, f32[32,2,64]{2,1,0:T(2,128)S(1)} %get-tuple-element.22, pred[64,64]{0,1:T(8,128)(4,1)S(1)} %iota_compare_fusion), kind=kOutput, calls=%fused_computation.24 | convolution fusion | flops 71307328 | bytes 4739072 | tf_op jit(solution)/shard_map/vmap(hqk,khd->qhd)/dot_general | solution.py:91
  219.1 3.2 fusion.19
  222.4 0.8 add_convert_fusion.1
  223.2 0.4 copy-done.1
  223.6 0.4 add_convert_fusion.3
  224.1 0.6 pad_maximum_fusion.1
  224.7 1.1 copy.24
  225.8 0.4 copy-done.3
  226.1 7.9 %fusion.26 = f32[2048,2304]{1,0:T(8,128)} fusion(bf16[2304,512]{1,0:T(8,128)(2,1)S(1)} %copy-done.3, bf16[256,8,2,128]{3,2,1,0:T(2,128)(2,1)S(1)} %bitcast.61), kind=kOutput, calls=%fused_computation.54 | convolution fusion | flops 2415919104 | bytes 21102592 | tf_op jit(solution)/shard_map/dot_general | solution.py:179
  234.1 7.9 %fusion.36 = f32[2048,2304]{1,0:T(8,128)} fusion(bf16[2048,64]{1,0:T(8,128)(2,1)S(1)} %bitcast.68, bf16[2048,64]{1,0:T(8,128)(2,1)S(1)} %bitcast.66, bf16[2304,512]{1,0:T(8,128)(2,1)S(1)} %copy-done.3), kind=kOutput, calls=%fused_computation.65 | convolution fusion | flops 1209008128 | bytes 20512768 | tf_op jit(solution)/shard_map/dot_general | solution.py:179
  242.0 17.2 %add_convert_fusion = bf16[2048,2304]{1,0:T(8,128)(2,1)} fusion(f32[2048,2304]{1,0:T(8,128)} %fusion.26, f32[2048,2304]{1,0:T(8,128)} %fusion.36, bf16[2048,128]{1,0:T(8,128)(2,1)} %bitcast.72, bf16[2304,512]{1,0:T(8,128)(2,1)S(1)} %copy-done.3), kind=kOutput, calls=%fused_computation.1 | convolution fusion | flops 1222115328 | bytes 48300032 | tf_op jit(solution)/shard_map/dot_general | solution.py:179
  259.2 0.0 reduce-scatter.2.cloned.1.call-update
  259.2 0.0 copy-start.12
  259.2 0.1 copy.45
  259.4 0.9 copy-done.5
  260.2 0.2 copy-done.7
  260.4 0.2 copy-done.12
  260.6 11.8 %convolution_convert_fusion = bf16[2304,512]{1,0:T(8,128)(2,1)} fusion(bf16[2048,2304]{1,0:T(8,128)(2,1)} %all-gather.3.cloned.1.call-done, bf16[2048,128]{1,0:T(8,128)(2,1)S(1)} %bitcast.73, bf16[2048,64]{1,0:T(8,128)(2,1)S(1)} %bitcast.69, bf16[2048,64]{1,0:T(8,128)(2,1)S(1)} %bitcast.67, bf16[2048,256]{1,0:T(8,128)(2,1)S(1)} %bitcast.71), kind=kOutput, calls=%fused_computation.3 | convolution fusion | flops 4841406464 | bytes 13893632 | tf_op jit(solution)/shard_map/dot_general | solution.py:161
  272.4 7.4 %all-to-all-start = ((bf16[16,144,512]{2,1,0:T(8,128)(2,1)}), bf16[16,144,512]{2,1,0:T(8,128)(2,1)S(1)}, u32[]{:S(2)}, u32[]{:S(2)}) async-start(bf16[16,144,512]{2,1,0:T(8,128)(2,1)} %bitcast.65), calls=%async_computation.1 | async-start | bytes 4718592 | tf_op jit(solution)/shard_map/all_to_all | solution.py:33
  279.8 2.5 fusion.18
  282.3 1.1 copy.21
  283.4 1.1 copy.46
  284.5 108.6 %all-to-all-done = bf16[16,144,512]{2,1,0:T(8,128)(2,1)S(1)} async-done(((bf16[16,144,512]{2,1,0:T(8,128)(2,1)}), bf16[16,144,512]{2,1,0:T(8,128)(2,1)S(1)}, u32[]{:S(2)}, u32[]{:S(2)}) %all-to-all-start) | async-done | bytes 2359328 | tf_op jit(solution)/shard_map/all_to_all | solution.py:33
  393.1 0.3 convert_reduce_fusion
  393.5 0.7 slice.52
  394.1 0.7 fusion.73
  394.8 1.5 fusion.25
  396.3 16.0 %psum.35 = f32[2304]{0:T(1024)S(1)} all-reduce(f32[2304]{0:T(1024)S(1)} %get-tuple-element.6), channel_id=1, replica_groups=mesh['dp_0'=4,'dp_1'=2,'dp_2'=2,'tensor_0'=2,'tensor_1'=8] {'dp_0'}, use_global_device_ids=true, to_apply=%region_7.8 | all-reduce | flops 2304 | bytes 18432 | tf_op jit(solution)/shard_map/psum | solution.py:38
  412.3 11.9 %psum.36 = f32[2304]{0:T(1024)S(1)} all-reduce(f32[2304]{0:T(1024)S(1)} %psum.35), channel_id=1, replica_groups=mesh['dp_0'=4,'dp_1'=2,'dp_2'=2,'tensor_0'=2,'tensor_1'=8] {'dp_1'}, use_global_device_ids=true, to_apply=%region_8.9 | all-reduce | flops 2304 | bytes 18432 | tf_op jit(solution)/shard_map/psum | solution.py:38
  424.2 3.3 psum.37
  427.5 7.7 %psum.38 = f32[2304]{0:T(1024)S(1)} all-reduce(f32[2304]{0:T(1024)S(1)} %psum.37), channel_id=1, replica_groups=mesh['dp_0'=4,'dp_1'=2,'dp_2'=2,'tensor_0'=2,'tensor_1'=8] {'tensor_0'}, use_global_device_ids=true, to_apply=%region_10.11 | all-reduce | flops 2304 | bytes 18432 | tf_op jit(solution)/shard_map/psum | solution.py:38
  435.2 27.2 %psum.39 = f32[2304]{0:T(1024)} all-reduce(f32[2304]{0:T(1024)S(1)} %psum.38), channel_id=1, replica_groups=mesh['dp_0'=4,'dp_1'=2,'dp_2'=2,'tensor_0'=2,'tensor_1'=8] {'tensor_1'}, use_global_device_ids=true, to_apply=%region_11.12 | all-reduce | flops 2304 | bytes 18432 | tf_op jit(solution)/shard_map/psum | solution.py:38
  462.4 2.3 fusion.21
  (32 shorter events, 0.1 us)
Async XLA Ops:
  7.2 5.2 %copy-start.11 = (bf16[2048,256]{1,0:T(8,128)(2,1)S(1)}, bf16[2048,256]{1,0:T(8,128)(2,1)}, u32[]{:S(2)}) copy-start(bf16[2048,256]{1,0:T(8,128)(2,1)} %param.7) | copy-start | bytes 3145732
  7.2 57.9 %all-gather.5.cloned.1.call-start = ((), (), s32[]{:S(2)}) async-start(), calls=%async_computation.3 | async-start | bytes 2506752 | tf_op jit(solution)/shard_map/all_gather | solution.py:22
  8.9 171.0 %all-gather.3.cloned.1.call-start = ((), (), s32[]{:S(2)}) async-start(), calls=%async_computation.2 | async-start | bytes 10027008 | tf_op jit(solution)/shard_map/all_gather | solution.py:115
  12.4 382.4 %reduce-scatter.2.cloned.1.call-start = ((), (), s32[]{:S(2)}) async-start(), calls=%async_computation.4 | async-start | bytes 10027008 | tf_op jit(solution)/shard_map/reduce_scatter | solution.py:182
  190.1 2.5 copy-start.2
  190.1 9.6 %slice-start = ((s8[9437184]{0:T(1024)(128)(4,1)}), s8[4194304]{0:T(1024)(128)(4,1)S(1)}, s32[]{:S(2)}) async-start(s8[9437184]{0:T(1024)(128)(4,1)} %bitcast.76), calls=%async_computation.5 | async-start | bytes 8388608
  192.6 7.1 %slice-start.1 = ((s8[9437184]{0:T(1024)(128)(4,1)}), s8[4194304]{0:T(1024)(128)(4,1)S(1)}, s32[]{:S(2)}) async-start(s8[9437184]{0:T(1024)(128)(4,1)} %bitcast.76), calls=%async_computation.6 | async-start | bytes 8388608
  192.6 7.1 %slice-start.2 = ((s8[9437184]{0:T(1024)(128)(4,1)}), s8[1048576]{0:T(1024)(128)(4,1)S(1)}, s32[]{:S(2)}) async-start(s8[9437184]{0:T(1024)(128)(4,1)} %bitcast.76), calls=%async_computation.7 | async-start | bytes 2097152
  199.7 4.2 copy-start.15
  202.4 0.8 copy-start.13
  203.1 3.5 copy-start.8
  203.9 2.7 copy-start.9
  203.9 2.7 copy-start.10
  222.4 1.2 copy-start.1
  224.0 10.0 %copy-start.4 = (bf16[32,64,1,64]{3,1,0,2:T(8,128)(2,1)}, bf16[32,64,1,64]{3,1,0,2:T(8,128)(2,1)S(1)}, u32[]{:S(2)}) copy-start(bf16[32,64,1,64]{3,1,0,2:T(8,128)(2,1)S(1)} %get-tuple-element.14) | copy-start | bytes 786436
  224.0 10.0 %copy-start.6 = (bf16[32,64,1,64]{3,1,0,2:T(8,128)(2,1)}, bf16[32,64,1,64]{3,1,0,2:T(8,128)(2,1)S(1)}, u32[]{:S(2)}) copy-start(bf16[32,64,1,64]{3,1,0,2:T(8,128)(2,1)S(1)} %get-tuple-element.15) | copy-start | bytes 786436
  224.1 2.0 copy-start.3
  259.2 1.0 copy-start.5
  259.2 1.2 copy-start.7
  259.2 1.3 copy-start.12
  272.4 7.4 %copy-start.14 = (bf16[2048,128]{1,0:T(8,128)(2,1)S(1)}, bf16[2048,128]{1,0:T(8,128)(2,1)}, u32[]{:S(2)}) copy-start(bf16[2048,128]{1,0:T(8,128)(2,1)} %copy-done.13) | copy-start | bytes 1572868
  272.4 120.7 %all-to-all-start = ((bf16[16,144,512]{2,1,0:T(8,128)(2,1)}), bf16[16,144,512]{2,1,0:T(8,128)(2,1)S(1)}, u32[]{:S(2)}, u32[]{:S(2)}) async-start(bf16[16,144,512]{2,1,0:T(8,128)(2,1)} %bitcast.65), calls=%async_computation.1 | async-start | bytes 4718592 | tf_op jit(solution)/shard_map/all_to_all | solution.py:33
  284.5 110.3 %copy-start = (bf16[128,2304]{1,0:T(8,128)(2,1)S(1)}, bf16[128,2304]{1,0:T(8,128)(2,1)}, u32[]{:S(2)}) copy-start(bf16[128,2304]{1,0:T(8,128)(2,1)} %param.6) | copy-start | bytes 1769476
  284.5 110.3 %copy-start.16 = (f32[2304]{0:T(1024)S(1)}, f32[2304]{0:T(1024)}, u32[]{:S(2)}) copy-start(f32[2304]{0:T(1024)} %param.8) | copy-start | bytes 27652
Sparse Core Ops, SparseCore 0:
  11.3 53.7 all-gather.4
  67.4 112.4 all-gather.2
  259.3 109.5 reduce-scatter.1
where the time goes:
time: 472 us; the launch traced here: 471 us
  waiting for transfers between devices  276 us (58%)
  matrix products  83.3 us (18%)
  blocking collectives  66.1 us (14%)
  between operations  14.1 us (3%)
  other arithmetic  12.6 us (3%)
  local copies, waits for them, and re-layouts  11.9 us (3%)
  starting transfers between devices  7.51 us (2%)
    all_gather x1, waiting for transfers between devices, per_device(): gathered = lax.all_gather(normed_input, TENSOR, axis=0, tiled=True)  115 us
    all_to_all x1, waiting for transfers between devices, sum_at_owner(): lax.all_to_all(split_up(value, dim, devices), axis, 0, 0, tiled=True)  109 us
    psum x5, blocking collectives, one_axis_at_a_time(): return functools.reduce(lax.psum, axes, value)  66.1 us
    all_gather x1, waiting for transfers between devices, in_one_piece(): result = lax.all_gather(both, axis, axis=dim, tiled=True)  52.2 us
    dot_general x3, matrix products, per_device(): lax.dot_general(block, weight, contract_last, preferred_element_type=jnp....  33.1 us
    dot_general x3, matrix products, per_device(): jnp.dot(gathered, piece, preferred_element_type=jnp.float32)  16.9 us
    dot_general x1, matrix products, per_device(): lax.dot_general(block, joined, contract_first, preferred_element_type=jnp...  11.8 us
  transfers between devices with their start and end apart: 4, of which 3 were waited for; matrix products, arithmetic and copies ran while one was open for 5% of the time, Pallas kernels for 0%

commit v1 on v0

--- a/solution.py
+++ b/solution.py
@@ -112,7 +112,9 @@
     inv_one = lax.rsqrt(jnp.mean(rows_f * rows_f, -1, keepdims=True) + EPS)
     unit_one = rows_f * inv_one
     normed_input = (unit_one * pre_gain).astype(jnp.bfloat16)
-    gathered = lax.all_gather(normed_input, TENSOR, axis=0, tiled=True)
+    gathered = jnp.concatenate(
+        lax.all_to_all(jnp.stack([normed_input] * lax.axis_size(TENSOR)), TENSOR, 0, 0), axis=0
+    )
     segment_length = gathered.shape[0]
     token_span = SEQ_LEN
     pieces_count = segment_length // token_span

time: 472 us -> 530 us (1.12)
  waiting for transfers between devices: 276 us -> 322 us
  starting transfers between devices: 7.51 us -> 17.1 us
    all_to_all x0 -> x1, waiting for transfers between devices: none -> 140 us  [per_device(): lax.all_to_all(jnp.stack([normed_input] * lax.axis_size(TENSOR)), TENSOR,...]
    all_gather x1 -> x0, waiting for transfers between devices: 115 us -> none  [per_device(): gathered = lax.all_gather(normed_input, TENSOR, axis=0, tiled=True)]
    all_gather x1, waiting for transfers between devices: 52.2 us -> 65.9 us  [in_one_piece(): result = lax.all_gather(both, axis, axis=dim, tiled=True)]
    all_to_all x0 -> x1, starting transfers between devices: none -> 9.39 us  [per_device(): lax.all_to_all(jnp.stack([normed_input] * lax.axis_size(TENSOR)), TENSOR,...]
    all_to_all x1, waiting for transfers between devices: 109 us -> 116 us  [sum_at_owner(): lax.all_to_all(split_up(value, dim, devices), axis, 0, 0, tiled=True)]
  transfers between devices with their start and end apart: 4 -> 4, of which waited for: 3 -> 3; matrix products, arithmetic and copies ran while one was open for 5% -> 4% of each run, Pallas kernels for 0% -> 0%
where the time goes in v1:
time: 530 us; the launch traced here: 529 us
  waiting for transfers between devices  322 us (61%)
  matrix products  83.4 us (16%)
  blocking collectives  65.9 us (12%)
  starting transfers between devices  17.1 us (3%)
  local copies, waits for them, and re-layouts  15.4 us (3%)
  between operations  14.4 us (3%)
  other arithmetic  10.8 us (2%)
    all_to_all x1, waiting for transfers between devices, per_device(): lax.all_to_all(jnp.stack([normed_input] * lax.axis_size(TENSOR)), TENSOR,...  140 us
    all_to_all x1, waiting for transfers between devices, sum_at_owner(): lax.all_to_all(split_up(value, dim, devices), axis, 0, 0, tiled=True)  116 us
    all_gather x1, waiting for transfers between devices, in_one_piece(): result = lax.all_gather(both, axis, axis=dim, tiled=True)  65.9 us
    psum x5, blocking collectives, one_axis_at_a_time(): return functools.reduce(lax.psum, axes, value)  65.9 us
    dot_general x3, matrix products, per_device(): lax.dot_general(block, weight, contract_last, preferred_element_type=jnp....  33.1 us
    dot_general x3, matrix products, per_device(): jnp.dot(gathered, piece, preferred_element_type=jnp.float32)  17.4 us
    dot_general x1, matrix products, per_device(): lax.dot_general(block, joined, contract_first, preferred_element_type=jnp...  11.8 us
  transfers between devices with their start and end apart: 4, of which 3 were waited for; matrix products, arithmetic and copies ran while one was open for 4% of the time, Pallas kernels for 0%

profile of v1, /device:TPU:4, one launch (start us, length us, event | category | flops | bytes accessed | tf_op | source)
XLA Modules:
  0.0 529.1 jit_solution(11373758624215268763)
XLA Ops:
  7.2 1.3 fusion.24
  8.4 1.3 fusion.22
  9.7 4.5 stack.2
  14.3 9.4 %all-to-all-start = ((bf16[16,128,2304]{2,1,0:T(8,128)(2,1)}), bf16[16,128,2304]{2,1,0:T(8,128)(2,1)}, u32[]{:S(2)}, u32[]{:S(2)}) async-start(bf16[16,128,2304]{2,1,0:T(8,128)(2,1)} %stack.2), calls=%async_computation | async-start | bytes 18874368 | tf_op jit(solution)/shard_map/all_to_all | solution.py:116
  23.7 0.0 all-gather.2.cloned.1.call-start
  23.7 0.0 copy-done.17
  23.7 0.0 copy-done.18
  23.7 0.0 copy-done.19
  23.7 0.7 pad_maximum_fusion.5
  24.4 0.0 all-gather.2.cloned.1.call-update
  24.4 0.0 reduce-scatter.2.cloned.1.call-start
  24.5 0.3 reshape.143
  24.8 0.1 fusion.52
  25.0 65.9 %all-gather.2.cloned.1.call-done = bf16[2304,512]{1,0:T(8,128)(2,1)} async-done(((bf16[144,512]{1,0:T(8,128)(2,1)}), bf16[2304,512]{1,0:T(8,128)(2,1)}) %all-gather.2.cloned.1.call-update) | async-done | bytes 2359312 | tf_op jit(solution)/shard_map/all_gather | solution.py:22
  90.9 1.3 slice_bitcast_fusion
  92.3 1.6 copy.29
  93.8 139.9 %all-to-all-done = bf16[16,128,2304]{2,1,0:T(8,128)(2,1)} async-done(((bf16[16,128,2304]{2,1,0:T(8,128)(2,1)}), bf16[16,128,2304]{2,1,0:T(8,128)(2,1)}, u32[]{:S(2)}, u32[]{:S(2)}) %all-to-all-start) | async-done | bytes 9437216 | tf_op jit(solution)/shard_map/all_to_all | solution.py:116
  233.7 5.7 %fusion.72 = f32[32,64,2,128]{3,1,2,0:T(8,128)S(1)} fusion(bf16[32,64,2304,1]{2,1,3,0:T(8,128)(2,1)} %bitcast.3, bf16[2,128,2304,1]{2,1,0,3:T(8,128)(2,1)} %bitcast.87), kind=kOutput, calls=%fused_computation.103 | convolution fusion | flops 2415919104 | bytes 12713984 | tf_op jit(solution)/shard_map/dot_general | solution.py:125
  239.4 0.0 copy-start.1
  239.4 0.7 subtract_convert_fusion.1
  240.1 0.0 copy-start.9
  240.1 0.0 copy-start.10
  240.1 0.9 copy-done.1
  241.0 5.2 convolution_bitcast_fusion.3
  246.2 0.5 fusion.34
  246.7 0.3 pad_maximum_fusion.2
  247.0 6.5 %convolution_convert_fusion.2 = bf16[32,64,128]{2,1,0:T(8,128)(2,1)S(1)} fusion(bf16[32,64,2304]{2,1,0:T(8,128)(2,1)} %bitcast, bf16[2304,512]{1,0:T(8,128)(2,1)S(1)} %copy-done.1), kind=kOutput, calls=%fused_computation.40 | convolution fusion | flops 1208221696 | bytes 10551296 | tf_op jit(solution)/shard_map/dot_general | solution.py:125
  253.5 0.0 copy-start.13
  253.5 0.7 fusion.30
  254.2 2.6 fusion.13
  256.9 6.2 %convolution_bitcast_fusion.2 = f32[32,64,1,128]{3,1,0,2:T(8,128)} fusion(f32[32,2,64,64]{3,2,1,0:T(8,128)S(1)} %fusion.30, f32[32,2,64,64]{2,3,1,0:T(8,128)} %get-tuple-element.21, bf16[32,64,2,64]{3,1,2,0:T(8,128)(2,1)} %copy-done.10, bf16[32,64,2,64]{3,1,2,0:T(8,128)(2,1)} %copy-done.9, f32[32,2,64]{2,1,0:T(2,128)S(1)} %get-tuple-element.20, ...), kind=kOutput, calls=%fused_computation.37 | convolution fusion | flops 73404480 | bytes 4214784 | tf_op jit(solution)/shard_map/vmap(hqk,qhd->khd)/dot_general | solution.py:92
  263.1 5.9 %convolution_bitcast_fusion = f32[32,64,2,128]{3,1,2,0:T(8,128)S(1)} fusion(f32[32,2,64,64]{3,2,1,0:T(8,128)} %copy-done.8, f32[32,2,64,64]{2,3,1,0:T(8,128)} %get-tuple-element.21, bf16[32,64,128]{2,1,0:T(8,128)(2,1)} %copy-done.15, f32[32,2,64]{2,1,0:T(2,128)S(1)} %get-tuple-element.20, pred[64,64]{0,1:T(8,128)(4,1)S(1)} %iota_compare_fusion), kind=kOutput, calls=%fused_computation.23 | convolution fusion | flops 71307328 | bytes 4739072 | tf_op jit(solution)/shard_map/vmap(hqk,khd->qhd)/dot_general | solution.py:91
  269.1 3.2 fusion.19
  272.3 0.8 add_convert_fusion.1
  273.1 0.4 copy-done.3
  273.5 0.4 add_convert_fusion.3
  274.0 0.6 pad_maximum_fusion.1
  274.6 1.1 copy.22
  275.7 0.4 copy-done.2
  276.0 8.0 %fusion.26 = f32[2048,2304]{1,0:T(8,128)} fusion(bf16[2304,512]{1,0:T(8,128)(2,1)S(1)} %copy-done.2, bf16[256,8,2,128]{3,2,1,0:T(2,128)(2,1)S(1)} %bitcast.79), kind=kOutput, calls=%fused_computation.55 | convolution fusion | flops 2415919104 | bytes 21102592 | tf_op jit(solution)/shard_map/dot_general | solution.py:181
  284.0 7.9 %fusion.36 = f32[2048,2304]{1,0:T(8,128)} fusion(bf16[2048,64]{1,0:T(8,128)(2,1)S(1)} %bitcast.85, bf16[2048,64]{1,0:T(8,128)(2,1)S(1)} %bitcast.83, bf16[2304,512]{1,0:T(8,128)(2,1)S(1)} %copy-done.2), kind=kOutput, calls=%fused_computation.67 | convolution fusion | flops 1209008128 | bytes 20512768 | tf_op jit(solution)/shard_map/dot_general | solution.py:181
  291.9 17.2 %add_convert_fusion = bf16[2048,2304]{1,0:T(8,128)(2,1)} fusion(f32[2048,2304]{1,0:T(8,128)} %fusion.26, f32[2048,2304]{1,0:T(8,128)} %fusion.36, bf16[2048,128]{1,0:T(8,128)(2,1)} %bitcast.90, bf16[2304,512]{1,0:T(8,128)(2,1)S(1)} %copy-done.2), kind=kOutput, calls=%fused_computation.1 | convolution fusion | flops 1222115328 | bytes 48300032 | tf_op jit(solution)/shard_map/dot_general | solution.py:181
  309.1 0.0 reduce-scatter.2.cloned.1.call-update
  309.2 0.0 copy-start.12
  309.2 0.1 copy.39
  309.3 0.9 copy-done.5
  310.2 0.2 copy-done.7
  310.3 0.2 copy-done.12
  310.5 11.8 %convolution_convert_fusion = bf16[2304,512]{1,0:T(8,128)(2,1)} fusion(bf16[2048,2304]{1,0:T(8,128)(2,1)} %bitcast.22, bf16[2048,128]{1,0:T(8,128)(2,1)S(1)} %bitcast.91, bf16[2048,64]{1,0:T(8,128)(2,1)S(1)} %bitcast.86, bf16[2048,64]{1,0:T(8,128)(2,1)S(1)} %bitcast.84, bf16[2048,256]{1,0:T(8,128)(2,1)S(1)} %bitcast.89), kind=kOutput, calls=%fused_computation.3 | convolution fusion | flops 4841406464 | bytes 13893632 | tf_op jit(solution)/shard_map/dot_general | solution.py:163
  322.4 7.6 %all-to-all-start.1 = ((bf16[16,144,512]{2,1,0:T(8,128)(2,1)}), bf16[16,144,512]{2,1,0:T(8,128)(2,1)S(1)}, u32[]{:S(2)}, u32[]{:S(2)}) async-start(bf16[16,144,512]{2,1,0:T(8,128)(2,1)} %bitcast.82), calls=%async_computation.2 | async-start | bytes 4718592 | tf_op jit(solution)/shard_map/all_to_all | solution.py:33
  329.9 2.4 fusion.18
  332.4 1.1 copy.19
  333.5 1.1 copy.40
  334.6 116.3 %all-to-all-done.1 = bf16[16,144,512]{2,1,0:T(8,128)(2,1)S(1)} async-done(((bf16[16,144,512]{2,1,0:T(8,128)(2,1)}), bf16[16,144,512]{2,1,0:T(8,128)(2,1)S(1)}, u32[]{:S(2)}, u32[]{:S(2)}) %all-to-all-start.1) | async-done | bytes 2359328 | tf_op jit(solution)/shard_map/all_to_all | solution.py:33
  450.9 0.3 convert_reduce_fusion
  451.2 0.7 slice.52
  451.9 0.7 fusion.71
  452.5 1.5 fusion.25
  454.1 16.0 %psum.35 = f32[2304]{0:T(1024)S(1)} all-reduce(f32[2304]{0:T(1024)S(1)} %get-tuple-element.6), channel_id=1, replica_groups=mesh['dp_0'=4,'dp_1'=2,'dp_2'=2,'tensor_0'=2,'tensor_1'=8] {'dp_0'}, use_global_device_ids=true, to_apply=%region_7.8 | all-reduce | flops 2304 | bytes 18432 | tf_op jit(solution)/shard_map/psum | solution.py:38
  470.0 11.9 %psum.36 = f32[2304]{0:T(1024)S(1)} all-reduce(f32[2304]{0:T(1024)S(1)} %psum.35), channel_id=1, replica_groups=mesh['dp_0'=4,'dp_1'=2,'dp_2'=2,'tensor_0'=2,'tensor_1'=8] {'dp_1'}, use_global_device_ids=true, to_apply=%region_8.9 | all-reduce | flops 2304 | bytes 18432 | tf_op jit(solution)/shard_map/psum | solution.py:38
  481.9 3.3 psum.37
  485.2 7.7 %psum.38 = f32[2304]{0:T(1024)S(1)} all-reduce(f32[2304]{0:T(1024)S(1)} %psum.37), channel_id=1, replica_groups=mesh['dp_0'=4,'dp_1'=2,'dp_2'=2,'tensor_0'=2,'tensor_1'=8] {'tensor_0'}, use_global_device_ids=true, to_apply=%region_10.11 | all-reduce | flops 2304 | bytes 18432 | tf_op jit(solution)/shard_map/psum | solution.py:38
  492.9 27.0 %psum.39 = f32[2304]{0:T(1024)} all-reduce(f32[2304]{0:T(1024)S(1)} %psum.38), channel_id=1, replica_groups=mesh['dp_0'=4,'dp_1'=2,'dp_2'=2,'tensor_0'=2,'tensor_1'=8] {'tensor_1'}, use_global_device_ids=true, to_apply=%region_11.12 | all-reduce | flops 2304 | bytes 18432 | tf_op jit(solution)/shard_map/psum | solution.py:38
  520.0 2.3 fusion.21
  (31 shorter events, 0.1 us)
Async XLA Ops:
  14.3 9.5 %copy-start.17 = (bf16[144,256]{1,0:T(8,128)(2,1)S(1)}, bf16[144,256]{1,0:T(8,128)(2,1)}, u32[]{:S(2)}) copy-start(bf16[144,256]{1,0:T(8,128)(2,1)} %param.9) | copy-start | bytes 221188
  14.3 9.5 %copy-start.18 = (bf16[144,128]{1,0:T(8,128)(2,1)S(1)}, bf16[144,128]{1,0:T(8,128)(2,1)}, u32[]{:S(2)}) copy-start(bf16[144,128]{1,0:T(8,128)(2,1)} %param.11) | copy-start | bytes 110596
  14.3 9.5 %copy-start.19 = (bf16[144,128]{1,0:T(8,128)(2,1)S(1)}, bf16[144,128]{1,0:T(8,128)(2,1)}, u32[]{:S(2)}) copy-start(bf16[144,128]{1,0:T(8,128)(2,1)} %param.10) | copy-start | bytes 110596
  14.3 10.2 %copy-start.11 = (bf16[2048,256]{1,0:T(8,128)(2,1)S(1)}, bf16[2048,256]{1,0:T(8,128)(2,1)}, u32[]{:S(2)}) copy-start(bf16[2048,256]{1,0:T(8,128)(2,1)} %param.7) | copy-start | bytes 3145732
  14.3 219.4 %all-to-all-start = ((bf16[16,128,2304]{2,1,0:T(8,128)(2,1)}), bf16[16,128,2304]{2,1,0:T(8,128)(2,1)}, u32[]{:S(2)}, u32[]{:S(2)}) async-start(bf16[16,128,2304]{2,1,0:T(8,128)(2,1)} %stack.2), calls=%async_computation | async-start | bytes 18874368 | tf_op jit(solution)/shard_map/all_to_all | solution.py:116
  23.7 67.2 %all-gather.2.cloned.1.call-start = ((), (), s32[]{:S(2)}) async-start(), calls=%async_computation.3 | async-start | bytes 2506752 | tf_op jit(solution)/shard_map/all_gather | solution.py:22
  24.4 428.1 %reduce-scatter.2.cloned.1.call-start = ((), (), s32[]{:S(2)}) async-start(), calls=%async_computation.4 | async-start | bytes 10027008 | tf_op jit(solution)/shard_map/reduce_scatter | solution.py:184
  239.4 1.7 copy-start.1
  240.1 14.1 %copy-start.9 = (bf16[32,64,2,64]{3,1,2,0:T(8,128)(2,1)}, bf16[32,64,2,64]{3,1,2,0:T(8,128)(2,1)S(1)}, u32[]{:S(2)}) copy-start(bf16[32,64,2,64]{3,1,2,0:T(8,128)(2,1)S(1)} %get-tuple-element.10) | copy-start | bytes 1572868
  240.1 14.1 %copy-start.10 = (bf16[32,64,2,64]{3,1,2,0:T(8,128)(2,1)}, bf16[32,64,2,64]{3,1,2,0:T(8,128)(2,1)S(1)}, u32[]{:S(2)}) copy-start(bf16[32,64,2,64]{3,1,2,0:T(8,128)(2,1)S(1)} %get-tuple-element.11) | copy-start | bytes 1572868
  247.0 7.2 %copy-start.15 = (bf16[32,64,128]{2,1,0:T(8,128)(2,1)}, bf16[32,64,128]{2,1,0:T(8,128)(2,1)S(1)}, u32[]{:S(2)}) copy-start(bf16[32,64,128]{2,1,0:T(8,128)(2,1)S(1)} %pad_maximum_fusion.2) | copy-start | bytes 1572868
  253.5 3.4 copy-start.13
  254.2 2.7 copy-start.8
  272.3 1.2 copy-start.3
  274.0 10.0 %copy-start.4 = (bf16[32,64,1,64]{3,1,0,2:T(8,128)(2,1)}, bf16[32,64,1,64]{3,1,0,2:T(8,128)(2,1)S(1)}, u32[]{:S(2)}) copy-start(bf16[32,64,1,64]{3,1,0,2:T(8,128)(2,1)S(1)} %get-tuple-element.12) | copy-start | bytes 786436
  274.0 10.0 %copy-start.6 = (bf16[32,64,1,64]{3,1,0,2:T(8,128)(2,1)}, bf16[32,64,1,64]{3,1,0,2:T(8,128)(2,1)S(1)}, u32[]{:S(2)}) copy-start(bf16[32,64,1,64]{3,1,0,2:T(8,128)(2,1)S(1)} %get-tuple-element.13) | copy-start | bytes 786436
  274.0 2.0 copy-start.2
  309.1 1.0 copy-start.5
  309.2 1.2 copy-start.7
  309.2 1.3 copy-start.12
  322.4 7.6 %copy-start.14 = (bf16[32,64,128]{2,1,0:T(8,128)(2,1)S(1)}, bf16[32,64,128]{2,1,0:T(8,128)(2,1)}, u32[]{:S(2)}) copy-start(bf16[32,64,128]{2,1,0:T(8,128)(2,1)} %copy-done.13) | copy-start | bytes 1572868
  322.4 128.5 %all-to-all-start.1 = ((bf16[16,144,512]{2,1,0:T(8,128)(2,1)}), bf16[16,144,512]{2,1,0:T(8,128)(2,1)S(1)}, u32[]{:S(2)}, u32[]{:S(2)}) async-start(bf16[16,144,512]{2,1,0:T(8,128)(2,1)} %bitcast.82), calls=%async_computation.2 | async-start | bytes 4718592 | tf_op jit(solution)/shard_map/all_to_all | solution.py:33
  334.6 117.9 %copy-start = (bf16[128,2304]{1,0:T(8,128)(2,1)S(1)}, bf16[128,2304]{1,0:T(8,128)(2,1)}, u32[]{:S(2)}) copy-start(bf16[128,2304]{1,0:T(8,128)(2,1)} %param.6) | copy-start | bytes 1769476
  334.6 117.9 %copy-start.16 = (f32[2304]{0:T(1024)S(1)}, f32[2304]{0:T(1024)}, u32[]{:S(2)}) copy-start(f32[2304]{0:T(1024)} %param.8) | copy-start | bytes 27652
Sparse Core Ops, SparseCore 0:
  27.8 63.0 all-gather.1
  309.3 117.3 reduce-scatter.1
